TPU v7x, 512 devices: a whole 4x8x8 slice. The times are simulated.
512 devices in a mesh: dp: 32 (over x, y), mx: 4 (over z_hi, core), my: 4 (over z_lo).
Axes of the slice: x: 4, y: 8, z: 8 (z_hi: 2, z_lo: 4; z = z_hi * 4 + z_lo), core: 2. Of those that a mesh axis runs over, the one named last changes fastest.
Arguments:
- mentor_final_states: bfloat16 [2048, 4608], P('dp'), may hold values from -12 to 12
- mentor_output_matrix: bfloat16 [4608, 4096], P(None, ('mx', 'my')), may hold values from -0.09375 to 0.09375
- learner_final_states: bfloat16 [2048, 3584], P('dp', 'mx'), may hold values from -12 to 12
- learner_output_matrix: bfloat16 [3584, 4096], P('mx', 'my'), may hold values from -0.09375 to 0.09375
- loss_mask: int32 [2048], P('dp'), may hold values 0 or 1
Outputs:
- mismatch_per_piece: float32 [2048], P('dp')
- mean_loss: float32 [], replicated
- student_grad: float32 [2048, 4096], P('dp', 'my')
All inputs are finite; a program needn't handle non-finite values.
Results may differ from a plain program's by a relative error of at most 0.0003.
Values sent between devices are 32-bit elements.
A program may use at most 64 MiB of HBM per device.

v0:
```python
import jax
import jax.numpy as jnp
from jax import lax
from jax.sharding import Mesh
from jax.sharding import PartitionSpec as P

DP = ("dp_0", "dp_1")


SOFTENING_HEAT = 2.0


def over_axes(array, axes):
    for axis in axes:
        array = lax.psum(array, axis)
    return array


def over_pieces(array, axis):
    blocks = lax.all_gather(array, axis)
    return blocks.sum(axis=0)


def merged(part, axis, combine):
    gathered = jax.tree.map(lambda a: lax.all_gather(a, axis), part)

    def take(source):
        return jax.tree.map(lambda a: lax.dynamic_index_in_dim(a, source, 0, False), gathered)

    return lax.fori_loop(
        1, lax.axis_size(axis), lambda source, state: combine(state, take(source)), take(0)
    )


def picked(array, axis, root):
    return lax.dynamic_index_in_dim(lax.all_gather(array, axis), root, 0, keepdims=False)


def row_stats(values):
    row_max = jnp.max(values, axis=1)
    row_sum = jnp.sum(jnp.exp(values - row_max[:, None]), axis=1)
    return (row_max, row_sum)


def join_stats(left_stat, right_stat):
    row_max = jnp.maximum(left_stat[0], right_stat[0])
    row_sum = left_stat[1] * jnp.exp(left_stat[0] - row_max) + right_stat[1] * jnp.exp(
        right_stat[0] - row_max
    )
    return (row_max, row_sum)


def local(
    mentor_final_states,
    mentor_output_matrix,
    learner_final_states,
    learner_output_matrix,
    loss_mask,
):
    groups = lax.axis_size(("mx", "my"))
    piece_cols = mentor_output_matrix.shape[1]
    lexicon_length = piece_cols * groups
    local_tokens = mentor_final_states.shape[0]
    piece_count = local_tokens * lax.axis_size(DP)
    global_multiplier = SOFTENING_HEAT * lexicon_length * piece_count
    mentor_softened_scores = (
        jnp.dot(mentor_final_states, mentor_output_matrix, preferred_element_type=jnp.float32)
        / SOFTENING_HEAT
    )
    learner_contribution = jnp.dot(
        learner_final_states, learner_output_matrix, preferred_element_type=jnp.float32
    )
    piece_importance = loss_mask.astype(jnp.float32)
    usable_count = over_axes(jnp.sum(piece_importance), DP)
    learner_softened_scores = over_pieces(learner_contribution, "mx") / SOFTENING_HEAT
    teacher_max, teacher_sum = merged(row_stats(mentor_softened_scores), ("mx", "my"), join_stats)
    student_max, student_sum = merged(row_stats(learner_softened_scores), "my", join_stats)
    mentor_logarithmic_odds = mentor_softened_scores - (teacher_max + jnp.log(teacher_sum))[:, None]
    learner_logarithmic_odds = (
        learner_softened_scores - (student_max + jnp.log(student_sum))[:, None]
    )
    outer_block = lax.all_gather(mentor_logarithmic_odds, "my", axis=1, tiled=True)
    aligned = picked(outer_block, "mx", lax.axis_index("my"))
    mentor_likelihoods = jnp.exp(aligned)
    partial_kl = jnp.sum(mentor_likelihoods * (aligned - learner_logarithmic_odds), axis=1)
    mismatch_per_piece = SOFTENING_HEAT * SOFTENING_HEAT * over_pieces(partial_kl, "my")
    prob_gap = jnp.exp(learner_logarithmic_odds) - mentor_likelihoods
    loss_sum = over_axes(jnp.sum(piece_importance * mismatch_per_piece), DP)
    mean_loss = loss_sum / usable_count
    multiplier = piece_importance * global_multiplier / usable_count
    student_grad = prob_gap * multiplier[:, None]
    return (mismatch_per_piece, mean_loss, student_grad)


def solution(mesh):
    split = Mesh(
        mesh.devices.reshape(4, 8, mesh.shape["mx"], mesh.shape["my"]), ("dp_0", "dp_1", "mx", "my")
    )
    in_specs = (P(DP, None), P(None, ("mx", "my")), P(DP, "mx"), P("mx", "my"), P(DP))
    out_specs = (P(DP), P(), P(DP, "my"))
    return jax.shard_map(local, mesh=split, in_specs=in_specs, out_specs=out_specs, check_vma=False)
```

profile of v0, /device:TPU:64, one launch (start us, length us, event | category | flops | bytes accessed | tf_op | source)
XLA Modules:
  0.0 154.1 jit_solution(621932956250404681)
XLA Ops:
  7.2 0.0 copy-start
  7.2 0.0 copy-start.1
  7.2 0.0 all-gather.12.cloned.1.call-start
  7.2 2.9 %fusion.7 = f32[64,1024]{1,0:T(8,128)} fusion(bf16[64,896]{1,0:T(8,128)(2,1)} %param.11, bf16[896,1024]{1,0:T(8,128)(2,1)} %param.12), kind=kOutput, calls=%fused_computation.29 | convolution fusion | flops 117440512 | bytes 2211840 | tf_op jit(solution)/shard_map/dot_general | solution.py:70
  10.1 0.0 all-gather.12.cloned.1.call-update
  10.1 0.0 all-gather.10.cloned.1.call-start
  10.2 0.0 copy-done
  10.2 0.0 copy-done.1
  10.2 0.6 fusion.6
  10.8 0.0 copy-start.2
  10.8 0.2 exponential_reduce_fusion.1
  11.0 1.3 dynamic-slice
  13.0 0.2 dynamic-update-slice
  13.2 0.2 dynamic-update-slice.1
  13.4 34.2 %all-reduce.5 = (f32[1024]{0:T(1024)S(1)}, f32[1024]{0:T(1024)S(1)}) all-reduce(f32[1024]{0:T(1024)S(1)} %dynamic-update-slice, f32[1024]{0:T(1024)S(1)} %dynamic-update-slice.1), channel_id=2, replica_groups=mesh['dp_0'=4,'dp_1'=8,'mx'=4,'my'=4] {'mx','my'}, use_global_device_ids=true, to_apply=%add | all-reduce | flops 2048 | bytes 16384
  47.7 0.1 reshape.11
  47.7 0.1 reshape.12
  47.8 0.7 while.34
  48.5 0.1 broadcast_subtract_fusion
  48.5 14.1 %all_gather.49 = f32[64,1024]{1,0:T(8,128)} all-gather(f32[64,256]{1,0:T(8,128)S(1)} %broadcast_subtract_fusion), channel_id=1, replica_groups=mesh['dp_0'=4,'dp_1'=8,'mx'=4,'my'=4] {'my'}, dimensions={1}, use_global_device_ids=true | all-gather | bytes 327680 | tf_op jit(solution)/shard_map/all_gather | solution.py:82
  62.6 0.0 all-gather.10.cloned.1.call-update
  62.7 1.3 dynamic-slice.2
  64.6 0.0 all-gather.12.cloned.1.call-done
  64.6 1.3 reduce_sum.64
  65.9 0.1 multiply_reduce_fusion
  66.1 0.2 dynamic-update-slice.2
  66.3 0.2 exponential_reduce_fusion
  66.5 0.2 dynamic-update-slice.3
  66.8 11.4 %all-reduce.7 = (f32[256]{0:T(256)S(1)}, f32[256]{0:T(256)S(1)}) all-reduce(f32[256]{0:T(256)S(1)} %dynamic-update-slice.2, f32[256]{0:T(256)S(1)} %dynamic-update-slice.3), channel_id=6, replica_groups=mesh['dp_0'=4,'dp_1'=8,'mx'=4,'my'=4] {'my'}, use_global_device_ids=true, to_apply=%add.2 | all-reduce | flops 512 | bytes 4096
  78.2 0.1 reshape.15
  78.3 0.1 reshape.16
  78.4 0.1 while.35
  78.5 22.0 %all-gather.10.cloned.1.call-done = f32[256,1024]{1,0:T(8,128)} async-done(((f32[64,1024]{1,0:T(8,128)}), f32[256,1024]{1,0:T(8,128)}) %all-gather.10.cloned.1.call-update) | async-done | bytes 1048592 | tf_op jit(solution)/shard_map/all_gather | solution.py:36
  100.5 1.2 fusion.5
  101.7 0.2 dynamic-update-slice.4
  101.9 10.2 %all-reduce.4 = f32[256]{0:T(256)S(1)} all-reduce(f32[256]{0:T(256)S(1)} %dynamic-update-slice.4), channel_id=8, replica_groups=mesh['dp_0'=4,'dp_1'=8,'mx'=4,'my'=4] {'my'}, use_global_device_ids=true, to_apply=%add.4 | all-reduce | flops 256 | bytes 2048
  112.1 0.1 reshape.17
  112.2 0.0 copy-done.2
  112.2 1.1 convert_reduce_fusion
  113.3 11.4 %all-reduce.8 = (f32[]{:T(128)}, f32[]{:T(128)}) all-reduce(f32[]{:T(128)} %get-tuple-element.274, f32[]{:T(128)} %get-tuple-element.273), channel_id=1, replica_groups=mesh['dp_0'=4,'dp_1'=8,'mx'=4,'my'=4] {'dp_0'}, use_global_device_ids=true, to_apply=%region_12.13 | all-reduce | flops 2 | bytes 16 | tf_op jit(solution)/shard_map/psum | solution.py:15
  124.7 17.7 %all-reduce.6 = (f32[]{:T(128)}, f32[]{:T(128)}) all-reduce(f32[]{:T(128)} %get-tuple-element.301, f32[]{:T(128)} %get-tuple-element.302), channel_id=1, replica_groups=mesh['dp_0'=4,'dp_1'=8,'mx'=4,'my'=4] {'dp_1'}, use_global_device_ids=true, to_apply=%region_13.14 | all-reduce | flops 2 | bytes 16 | tf_op jit(solution)/shard_map/psum | solution.py:15
  142.3 0.6 multiply_divide_fusion
  143.0 1.8 %subtract_multiply_fusion = f32[64,1024]{1,0:T(8,128)} fusion(f32[4,64,1024]{2,1,0:T(8,128)} %bitcast.49, s32[]{:T(128)S(6)} %select_n.32, f32[64,1024]{1,0:T(8,128)S(1)} %reduce_sum.64, f32[64]{0:T(128)S(1)} %multiply_divide_fusion, f32[64]{0:T(128)S(1)} %log_add_fusion), kind=kLoop, calls=%fused_computation.17 | loop fusion | flops 262144 | bytes 786948 | tf_op jit(solution)/shard_map/mul | solution.py:91
  (30 shorter events, 0.5 us)
Async XLA Ops:
  7.2 3.0 %copy-start = (bf16[4608,256]{1,0:T(8,128)(2,1)S(1)}, bf16[4608,256]{1,0:T(8,128)(2,1)}, u32[]{:S(2)}) copy-start(bf16[4608,256]{1,0:T(8,128)(2,1)} %param.10) | copy-start | bytes 7077892
  7.2 3.0 %copy-start.1 = (bf16[64,4608]{1,0:T(8,128)(2,1)S(1)}, bf16[64,4608]{1,0:T(8,128)(2,1)}, u32[]{:S(2)}) copy-start(bf16[64,4608]{1,0:T(8,128)(2,1)} %param.9) | copy-start | bytes 1769476
  7.2 57.4 %all-gather.12.cloned.1.call-start = ((), (), s32[]{:S(2)}) async-start(), calls=%async_computation.1 | async-start | bytes 1310720 | tf_op jit(solution)/shard_map/all_gather | solution.py:20
  10.1 90.4 %all-gather.10.cloned.1.call-start = ((), (), s32[]{:S(2)}) async-start(), calls=%async_computation | async-start | bytes 1310720 | tf_op jit(solution)/shard_map/all_gather | solution.py:36
  10.8 101.4 %copy-start.2 = (s32[64]{0:T(128)S(1)}, s32[64]{0:T(128)}, u32[]{:S(2)}) copy-start(s32[64]{0:T(128)} %param.13) | copy-start | bytes 772
Sparse Core Ops, SparseCore 0:
  10.7 39.6 all-gather.11
  62.8 37.6 all-gather.9
where the time goes:
time: 155 us; the launch traced here: 154 us
  blocking collectives  99 us (64%)
  waiting for transfers between devices  22.1 us (14%)
  between operations  18 us (12%)
  other arithmetic  7.11 us (5%)
  local copies, waits for them, and re-layouts  4.15 us (3%)
  matrix products  3.48 us (2%)
    unnamed x3, blocking collectives  55.8 us
    psum x2, blocking collectives, over_axes(): array = lax.psum(array, axis)  29 us
    all_gather x1, waiting for transfers between devices, picked(): lax.all_gather(array, axis)  22 us
    all_gather x1, blocking collectives, local(): lax.all_gather(mentor_logarithmic_odds, 'my', axis=1, tiled=True)  14.1 us
    unnamed x18, local copies, waits for them, and re-layouts  3.76 us
  transfers between devices with their start and end apart: 2, of which 1 were waited for; matrix products, arithmetic and copies ran while one was open for 4% of the time, Pallas kernels for 0%

commit v1 on v0

v1 whole, which is shorter than its diff:
```python
import functools

import jax
import jax.numpy as jnp
from jax import lax
from jax.experimental import pallas as pl
from jax.experimental.pallas import tpu as pltpu
from jax.sharding import Mesh
from jax.sharding import PartitionSpec as P

DP = ("dp_0", "dp_1")
MESH = pl.DeviceIdType.MESH
HEAT = 2.0
CHUNKS = 6


def kernel(
    sizes,
    scale,
    xt_hbm,
    wt_hbm,
    xs_hbm,
    ws_hbm,
    mask_ref,
    grad_ref,
    mis_ref,
    loss_ref,
    xt,
    wt,
    xs,
    ws,
    psend,
    precv,
    csum,
    recv1,
    gblk,
    stats,
    cnt_x,
    cnt_y,
    los_x,
    los_y,
    ld_sem,
    d_send,
    d_recv,
    p1_send,
    p1_recv,
    st_send,
    st_recv,
    g_send,
    g_recv,
    f_send,
    f_recv,
    x_send,
    x_recv,
    y_send,
    y_recv,
):
    nx, ny, nk, ni = sizes
    ix = lax.axis_index("dp_0")
    iy = lax.axis_index("dp_1")
    k = lax.axis_index("mx")
    i = lax.axis_index("my")
    c = lax.rem(k, 2)
    zh = lax.div(k, 2)
    partner = k + 1 - 2 * c
    tokens, width = csum.shape[1], csum.shape[2]
    deep = wt.shape[0] // CHUNKS

    barrier = pltpu.get_barrier_semaphore()
    peers = []
    for dk in range(nk):
        for di in range(ni):
            if dk or di:
                peers.append({"mx": lax.rem(k + dk, nk), "my": lax.rem(i + di, ni)})
    xpeers = [{"dp_0": lax.rem(ix + d, nx)} for d in range(1, nx)]
    ypeers = [{"dp_1": lax.rem(iy + d, ny)} for d in range(1, ny)]
    for peer in peers + xpeers + ypeers:
        pl.semaphore_signal(barrier, inc=1, device_id=peer, device_id_type=MESH)

    loads = [pltpu.make_async_copy(xs_hbm, xs, ld_sem.at[0])]
    order = [c, 2 + c, 1 - c, 3 - c]
    for n, j in enumerate(order):
        cols = pl.ds(pl.multiple_of(j * width, width), width)
        loads.append(pltpu.make_async_copy(ws_hbm.at[:, cols], ws.at[n], ld_sem.at[1 + n]))
    loads.append(pltpu.make_async_copy(xt_hbm, xt, ld_sem.at[5]))
    for n in range(CHUNKS):
        rows = pl.ds(n * deep, deep)
        loads.append(pltpu.make_async_copy(wt_hbm.at[rows], wt.at[rows], ld_sem.at[6 + n]))
    for copy in loads:
        copy.start()

    def student(n):
        loads[1 + n].wait()
        return jnp.dot(xs[...], ws[n], preferred_element_type=jnp.float32)

    def remote(src, dst, send, recv, peer):
        return pltpu.make_async_remote_copy(
            src_ref=src, dst_ref=dst, send_sem=send, recv_sem=recv, device_id=peer, device_id_type=MESH
        )

    mask = mask_ref[...].astype(jnp.float32)
    cnt_x[ix] = jnp.full((1, 128), jnp.sum(mask), jnp.float32)

    loads[0].wait()
    swaps = []
    for n in range(2):
        psend[n] = student(n)
        if n == 0:
            pl.semaphore_wait(barrier, len(peers + xpeers + ypeers))
        copy = remote(psend.at[n], precv.at[n], d_send.at[n], d_recv.at[n], {"mx": partner})
        copy.start()
        swaps.append(copy)

    def spread(buf, me, stage, send, recv, peer_list):
        copies = []
        for d, peer in enumerate(peer_list):
            copies.append(remote(buf.at[me], buf.at[me], send.at[stage, d], recv.at[stage, d], peer))
        for copy in copies:
            copy.start()
        return copies

    first = []
    for n in range(2):
        own = student(2 + n)
        swaps[n].wait_recv()
        csum[n] = own + precv[n]
        j = 2 * n + 1 - c
        copy = remote(csum.at[n], recv1.at[zh], p1_send.at[n], p1_recv.at[zh], {"mx": i, "my": j})
        copy.start()
        first.append(copy)

    cx = spread(cnt_x, ix, 0, x_send, x_recv, xpeers)

    loads[5].wait()
    acc = jnp.zeros((tokens, width), jnp.float32)
    for n in range(CHUNKS):
        loads[6 + n].wait()
        rows = pl.ds(n * deep, deep)
        acc = acc + jnp.dot(xt[:, rows], wt[rows, :], preferred_element_type=jnp.float32)
    t = acc * (1.0 / HEAT)
    t_max = jnp.max(t, axis=1, keepdims=True)
    t_exp = jnp.exp(t - t_max)
    t_sum = jnp.sum(t_exp, axis=1, keepdims=True)
    t_lse = t_max + jnp.log(t_sum)

    for copy in cx:
        copy.wait_recv()
    cnt_y[iy] = jnp.sum(cnt_x[...], axis=0)
    cy = spread(cnt_y, iy, 0, y_send, y_recv, ypeers)

    for h in range(2):
        pltpu.make_async_copy(recv1.at[h], recv1.at[h], p1_recv.at[h]).wait()
    s = (recv1[0] + recv1[1]) * (1.0 / HEAT)
    s_max = jnp.max(s, axis=1, keepdims=True)
    s_sum = jnp.sum(jnp.exp(s - s_max), axis=1, keepdims=True)
    s_lse = s_max + jnp.log(s_sum)
    gap = jnp.sum(t_exp * (t - s), axis=1, keepdims=True) / t_sum

    row_id = lax.broadcasted_iota(jnp.int32, (tokens, 2 * tokens), 0)
    lane_id = lax.broadcasted_iota(jnp.int32, (tokens, 2 * tokens), 1)
    low = lane_id < tokens
    eye2 = (lane_id == row_id) | (lane_id == row_id + tokens)
    me = k * ni + i
    both = jnp.where(eye2, jnp.where(low, t_lse, s_lse), 0.0)
    gaps = jnp.where(eye2, jnp.broadcast_to(gap, both.shape), 0.0)
    stats[me, 0:1] = jnp.sum(both, axis=0, keepdims=True)
    stats[me, 1:2] = jnp.sum(gaps, axis=0, keepdims=True)
    sts = []
    for d, peer in enumerate(peers):
        sts.append(remote(stats.at[me], stats.at[me], st_send.at[d], st_recv.at[d], peer))
    for copy in sts:
        copy.start()
    for copy in cy:
        copy.wait_recv()
    count = jnp.sum(cnt_y[...], axis=0)
    for copy in sts:
        copy.wait_recv()

    lse = [stats[g, 0:1] for g in range(nk * ni)]
    top = functools.reduce(jnp.maximum, lse)
    weights = [jnp.exp(v - top) for v in lse]
    total = functools.reduce(jnp.add, weights)
    z = top + jnp.log(total)
    num = functools.reduce(jnp.add, [w * stats[g, 1:2] for g, w in enumerate(weights)])
    zt = z[:, :tokens]
    zs = z[:, tokens:]
    kl = (HEAT * HEAT) * (num[:, :tokens] / total[:, :tokens] - zt + zs)
    mis_ref[...] = kl
    los_x[ix] = jnp.full((1, 128), jnp.sum(mask * kl), jnp.float32)
    lx = spread(los_x, ix, 1, x_send, x_recv, xpeers)

    eye = (
        lax.broadcasted_iota(jnp.int32, (tokens, tokens), 0)
        == lax.broadcasted_iota(jnp.int32, (tokens, tokens), 1)
    )

    def column(row):
        return jnp.sum(jnp.where(eye, row, 0.0), axis=1, keepdims=True)

    factor = column(mask * scale / count[:, :tokens])
    gblk[...] = (jnp.exp(s - column(zs)) - jnp.exp(t - column(zt))) * factor
    outs = []
    mycols = pl.ds(pl.multiple_of(i * width, width), width)
    r = 1 - lax.rem(i, 2)
    for h in range(2):
        outs.append(
            remote(gblk, grad_ref.at[:, mycols], g_send.at[h], g_recv.at[lax.div(i, 2)], {"mx": 2 * h + r, "my": k})
        )
    for copy in outs:
        copy.start()

    for copy in lx:
        copy.wait_recv()
    los_y[iy] = jnp.sum(los_x[...], axis=0)
    ly = spread(los_y, iy, 1, y_send, y_recv, ypeers)

    forwards = []
    for n in range(2):
        j = 2 * n + 1 - c
        cols = pl.ds(pl.multiple_of(j * width, width), width)
        block = grad_ref.at[:, cols]
        pltpu.make_async_copy(block, block, g_recv.at[n]).wait()
        copy = remote(block, block, f_send.at[n], f_recv.at[n], {"mx": partner})
        copy.start()
        forwards.append(copy)

    for copy in ly:
        copy.wait_recv()
    loss_ref[...] = jnp.sum(los_y[...], axis=0) / count
    for copy in forwards:
        copy.wait_recv()
    for copy in swaps + first + cx + cy + sts + lx + outs + ly + forwards:
        copy.wait_send()


def local(xt, wt, xs, ws, mask):
    nx, ny, nk, ni = (lax.axis_size(a) for a in ("dp_0", "dp_1", "mx", "my"))
    tokens, depth_t = xt.shape
    width = wt.shape[1]
    depth_s, span = ws.shape
    scale = HEAT * width * nk * ni * tokens * nx * ny
    f32 = jnp.float32
    dma = pltpu.SemaphoreType.DMA
    vmem = pl.BlockSpec(memory_space=pltpu.VMEM)
    hbm = pl.BlockSpec(memory_space=pl.ANY)
    grad, mis, loss = pl.pallas_call(
        functools.partial(kernel, (nx, ny, nk, ni), scale),
        out_shape=(
            jax.ShapeDtypeStruct((tokens, span), f32),
            jax.ShapeDtypeStruct((1, tokens), f32),
            jax.ShapeDtypeStruct((1, 128), f32),
        ),
        in_specs=[hbm, hbm, hbm, hbm, vmem],
        out_specs=(vmem, vmem, vmem),
        scratch_shapes=[
            pltpu.VMEM((tokens, depth_t), jnp.bfloat16),
            pltpu.VMEM((depth_t, width), jnp.bfloat16),
            pltpu.VMEM((tokens, depth_s), jnp.bfloat16),
            pltpu.VMEM((4, depth_s, width), jnp.bfloat16),
            pltpu.VMEM((2, tokens, width), f32),
            pltpu.VMEM((2, tokens, width), f32),
            pltpu.VMEM((2, tokens, width), f32),
            pltpu.VMEM((2, tokens, width), f32),
            pltpu.VMEM((tokens, width), f32),
            pltpu.VMEM((nk * ni, 2, 128), f32),
            pltpu.VMEM((nx, 1, 128), f32),
            pltpu.VMEM((ny, 1, 128), f32),
            pltpu.VMEM((nx, 1, 128), f32),
            pltpu.VMEM((ny, 1, 128), f32),
            dma((6 + CHUNKS,)),
            dma((2,)),
            dma((2,)),
            dma((2,)),
            dma((2,)),
            dma((nk * ni,)),
            dma((nk * ni,)),
            dma((2,)),
            dma((2,)),
            dma((2,)),
            dma((2,)),
            dma((2, nx)),
            dma((2, nx)),
            dma((2, ny)),
            dma((2, ny)),
        ],
        compiler_params=pltpu.CompilerParams(collective_id=0, has_side_effects=True),
    )(xt, wt, xs, ws, mask.reshape(1, tokens))
    return mis.reshape(tokens), loss[0, 0], grad


def solution(mesh):
    split = Mesh(
        mesh.devices.reshape(4, 8, mesh.shape["mx"], mesh.shape["my"]), ("dp_0", "dp_1", "mx", "my")
    )
    in_specs = (P(DP, None), P(None, ("mx", "my")), P(DP, "mx"), P("mx", "my"), P(DP))
    out_specs = (P(DP), P(), P(DP, "my"))
    return jax.shard_map(local, mesh=split, in_specs=in_specs, out_specs=out_specs, check_vma=False)
```

time: 155 us -> 42.8 us (0.28)
  the two profiles are of different devices: /device:TPU:64 before, /device:TPU:1 now
where the time goes in v1:
time: 42.8 us; the launch traced here: 42.6 us
  Pallas kernels  37.5 us (88%)
  local copies, waits for them, and re-layouts  2.8 us (7%)
  between operations  2.32 us (5%)
    pallas_call x1, Pallas kernels, local(): pl.pallas_call(functools.partial(kernel, (nx, ny, nk, ni), scale), out_sh...  37.5 us
    unnamed x2, local copies, waits for them, and re-layouts  2.8 us

profile of v1, /device:TPU:1, one launch (start us, length us, event | category | flops | bytes accessed | tf_op | source)
XLA Modules:
  0.0 42.6 jit_solution(15349533648280159623)
XLA Ops:
  0.6 37.5 %shard_map.76 = (f32[64,1024]{1,0:T(8,128)}, f32[1,64]{1,0:T(1,128)}, f32[1,128]{1,0:T(1,128)}) custom-call(bf16[64,4608]{1,0:T(8,128)(2,1)} %xt_hbm.1, bf16[4608,256]{1,0:T(8,128)(2,1)} %wt_hbm.1, bf16[64,896]{1,0:T(8,128)(2,1)} %xs_hbm.1, bf16[896,1024]{1,0:T(8,128)(2,1)} %ws_hbm.1, s32[1,64]{1,0:T(1,128)} %bitcast.4), custom_call_target="tpu_custom_call" | custom-call | tf_op jit(solution)/shard_map/pallas_call | solution.py:246
  38.1 1.1 %copy.11 = f32[64]{0:T(128)} copy(f32[64]{0:T(128)} %bitcast.6) | data formatting | bytes 512
  39.8 1.7 %copy.13 = f32[64,1024]{1,0:T(8,128)} copy(f32[64,1024]{1,0:T(8,128)} %get-tuple-element.14) | data formatting | bytes 524288

commit v2 on v1

--- a/solution.py
+++ b/solution.py
@@ -21,7 +21,7 @@
     wt_hbm,
     xs_hbm,
     ws_hbm,
-    mask_ref,
+    mask_hbm,
     grad_ref,
     mis_ref,
     loss_ref,
@@ -29,6 +29,7 @@
     wt,
     xs,
     ws,
+    mask_ref,
     psend,
     precv,
     csum,
@@ -86,6 +87,7 @@
     for n in range(CHUNKS):
         rows = pl.ds(n * deep, deep)
         loads.append(pltpu.make_async_copy(wt_hbm.at[rows], wt.at[rows], ld_sem.at[6 + n]))
+    loads.append(pltpu.make_async_copy(mask_hbm, mask_ref, ld_sem.at[6 + CHUNKS]))
     for copy in loads:
         copy.start()
 
@@ -97,9 +99,6 @@
         return pltpu.make_async_remote_copy(
             src_ref=src, dst_ref=dst, send_sem=send, recv_sem=recv, device_id=peer, device_id_type=MESH
         )
-
-    mask = mask_ref[...].astype(jnp.float32)
-    cnt_x[ix] = jnp.full((1, 128), jnp.sum(mask), jnp.float32)
 
     loads[0].wait()
     swaps = []
@@ -129,6 +128,9 @@
         copy.start()
         first.append(copy)
 
+    loads[-1].wait()
+    mask = mask_ref[...].astype(jnp.float32)
+    cnt_x[ix] = jnp.full((1, 128), jnp.sum(mask), jnp.float32)
     cx = spread(cnt_x, ix, 0, x_send, x_recv, xpeers)
 
     loads[5].wait()
@@ -233,6 +235,17 @@
         copy.wait_send()
 
 
+def finish(grad, mis, loss, grad_out, mis_out, loss_out, sem):
+    copies = [
+        pltpu.make_async_copy(src, dst, sem.at[n])
+        for n, (src, dst) in enumerate(((grad, grad_out), (mis, mis_out), (loss, loss_out)))
+    ]
+    for copy in copies:
+        copy.start()
+    for copy in copies:
+        copy.wait()
+
+
 def local(xt, wt, xs, ws, mask):
     nx, ny, nk, ni = (lax.axis_size(a) for a in ("dp_0", "dp_1", "mx", "my"))
     tokens, depth_t = xt.shape
@@ -242,21 +255,22 @@
     f32 = jnp.float32
     dma = pltpu.SemaphoreType.DMA
     vmem = pl.BlockSpec(memory_space=pltpu.VMEM)
-    hbm = pl.BlockSpec(memory_space=pl.ANY)
+    hbm = pl.BlockSpec(memory_space=pltpu.HBM)
     grad, mis, loss = pl.pallas_call(
         functools.partial(kernel, (nx, ny, nk, ni), scale),
         out_shape=(
-            jax.ShapeDtypeStruct((tokens, span), f32),
-            jax.ShapeDtypeStruct((1, tokens), f32),
-            jax.ShapeDtypeStruct((1, 128), f32),
+            pltpu.VMEM((tokens, span), f32),
+            pltpu.VMEM((1, tokens), f32),
+            pltpu.VMEM((1, 128), f32),
         ),
-        in_specs=[hbm, hbm, hbm, hbm, vmem],
+        in_specs=[hbm] * 5,
         out_specs=(vmem, vmem, vmem),
         scratch_shapes=[
             pltpu.VMEM((tokens, depth_t), jnp.bfloat16),
             pltpu.VMEM((depth_t, width), jnp.bfloat16),
             pltpu.VMEM((tokens, depth_s), jnp.bfloat16),
             pltpu.VMEM((4, depth_s, width), jnp.bfloat16),
+            pltpu.VMEM((1, tokens), jnp.int32),
             pltpu.VMEM((2, tokens, width), f32),
             pltpu.VMEM((2, tokens, width), f32),
             pltpu.VMEM((2, tokens, width), f32),
@@ -267,7 +281,7 @@
             pltpu.VMEM((ny, 1, 128), f32),
             pltpu.VMEM((nx, 1, 128), f32),
             pltpu.VMEM((ny, 1, 128), f32),
-            dma((6 + CHUNKS,)),
+            dma((7 + CHUNKS,)),
             dma((2,)),
             dma((2,)),
             dma((2,)),
@@ -283,8 +297,20 @@
             dma((2, ny)),
             dma((2, ny)),
         ],
-        compiler_params=pltpu.CompilerParams(collective_id=0, has_side_effects=True),
+        compiler_params=pltpu.CompilerParams(collective_id=0, has_side_effects=True, vmem_limit_bytes=63000000),
     )(xt, wt, xs, ws, mask.reshape(1, tokens))
+    grad, mis, loss = pl.pallas_call(
+        finish,
+        out_shape=(
+            jax.ShapeDtypeStruct((tokens, span), f32),
+            jax.ShapeDtypeStruct((1, tokens), f32),
+            jax.ShapeDtypeStruct((1, 128), f32),
+        ),
+        in_specs=[vmem] * 3,
+        out_specs=(hbm,) * 3,
+        scratch_shapes=[dma((3,))],
+        compiler_params=pltpu.CompilerParams(vmem_limit_bytes=1 << 20),
+    )(grad, mis, loss)
     return mis.reshape(tokens), loss[0, 0], grad
 
 

time: 42.8 us -> 37.7 us (0.88)
  local copies, waits for them, and re-layouts: 2.8 us -> 0 us
  between operations: 2.32 us -> 0.64 us
  Pallas kernels: 37.5 us -> 36.9 us
    unnamed x2 -> x0, local copies, waits for them, and re-layouts: 2.8 us -> none
    pallas_call x1, Pallas kernels: 37.5 us -> 36.2 us  [local(): pl.pallas_call(functools.partial(kernel, (nx, ny, nk, ni), scale), out_sh...]
    pallas_call x0 -> x1, Pallas kernels: none -> 0.74 us  [local(): pl.pallas_call(finish, out_shape=(jax.ShapeDtypeStruct((tokens, span), f3...]
where the time goes in v2:
time: 37.7 us; the launch traced here: 37.6 us
  Pallas kernels  36.9 us (98%)
  between operations  0.64 us (2%)
    pallas_call x1, Pallas kernels, local(): pl.pallas_call(functools.partial(kernel, (nx, ny, nk, ni), scale), out_sh...  36.2 us

profile of v2, /device:TPU:1, one launch (start us, length us, event | category | flops | bytes accessed | tf_op | source)
XLA Modules:
  0.0 37.6 jit_solution(7060401661420489448)
XLA Ops:
  0.6 36.2 %shard_map.76 = (f32[64,1024]{1,0:T(8,128)S(1)}, f32[1,64]{1,0:T(1,128)S(1)}, f32[1,128]{1,0:T(1,128)S(1)}) custom-call(bf16[64,4608]{1,0:T(8,128)(2,1)} %xt_hbm.1, bf16[4608,256]{1,0:T(8,128)(2,1)} %wt_hbm.1, bf16[64,896]{1,0:T(8,128)(2,1)} %xs_hbm.1, bf16[896,1024]{1,0:T(8,128)(2,1)} %ws_hbm.1, s32[1,64]{1,0:T(1,128)} %bitcast.4), custom_call_target="tpu_custom_call" | custom-call | tf_op jit(solution)/shard_map/pallas_call | solution.py:259
  36.9 0.7 %shard_map.77 = (f32[64,1024]{1,0:T(8,128)}, f32[1,64]{1,0:T(1,128)}, f32[1,128]{1,0:T(1,128)}) custom-call(f32[64,1024]{1,0:T(8,128)S(1)} %get-tuple-element.9.grad, f32[1,64]{1,0:T(1,128)S(1)} %get-tuple-element.10.mis, f32[1,128]{1,0:T(1,128)S(1)} %get-tuple-element.11.loss), custom_call_target="tpu_custom_call" | custom-call | tf_op jit(solution)/shard_map/pallas_call | solution.py:302
